TPU v7x, 32 devices: a whole 2x2x4 slice. The times are simulated.
32 devices in a mesh: grp: 2 (over y), gy: 4 (over z), gx: 2 (over x), gz: 2 (over core).
Axes of the slice: x: 2, y: 2, z: 4, core: 2. Of those that a mesh axis runs over, the one named last changes fastest.
Arguments:
- pair: bfloat16 [1024, 512, 128], P(('grp', 'gx', 'gz'), 'gy'), parts along dimension 0, may hold values from -6 to 6
- lengths: int32 [2], P('grp'), parts along dimension 0, may hold values from 256 to 512
- ln_gain: float32 [128], replicated, may hold values from 0.1 to 1.9
- ln_bias: float32 [128], replicated, may hold values from -3 to 3
- w_ab: bfloat16 [128, 512], replicated, may hold values from -0.5 to 0.5
- w_gate: bfloat16 [128, 128], replicated, may hold values from -0.5 to 0.5
- out_gain: float32 [128], replicated, may hold values from 0.1 to 1.9
- out_bias: float32 [128], replicated, may hold values from -3 to 3
- w_out: bfloat16 [128, 128], replicated, may hold values from -0.5 to 0.5
Outputs:
- update: bfloat16 [1024, 512, 128], P(('grp', 'gx', 'gz'), 'gy'), parts along dimension 0
There are 2 independent parts, one for each index of `grp`. A program takes and returns all parts, laid end to end along the dimension named above; an argument that names none is the same for every part. Nothing has to cross between parts.
Inputs may be any that keep to these rules, and one draw needn't show every extreme that they name: Residues from lengths[0] on are padding.
All inputs are finite; a program needn't handle non-finite values.
Results may differ from a plain program's by a relative error of at most 0.0052.
Values may be sent and summed in bfloat16 or wider, within the bound.
A program may use at most 128 MiB of HBM per device.

v0:
```python
import jax
import jax.numpy as jnp
from jax import lax
from jax.sharding import PartitionSpec as P


def layer_norm(values, gain, bias):
    values = values.astype(jnp.float32)
    mean = jnp.mean(values, -1, keepdims=True)
    spread = jnp.mean(jnp.square(values - mean), -1, keepdims=True)
    return (values - mean) * lax.rsqrt(spread + 1e-05) * gain + bias


def channel_norm(values, gain, bias):
    mean = jnp.mean(values, 0, keepdims=True)
    spread = jnp.mean(jnp.square(values - mean), 0, keepdims=True)
    return (values - mean) * lax.rsqrt(spread + 1e-05) * gain[:, None, None] + bias[:, None, None]


def body(pair, lengths, ln_gain, ln_bias, w_ab, w_gate, out_gain, out_bias, w_out):
    tile_rows, tile_cols, width = pair.shape
    hidden = w_out.shape[0]
    row_start = lax.axis_index(("gx", "gz")) * tile_rows
    col_index = lax.axis_index("gy")
    col_start = col_index * tile_cols
    normed = layer_norm(pair, ln_gain, ln_bias).astype(jnp.bfloat16)
    flat = normed.reshape(tile_rows * tile_cols, width)
    proj = jnp.dot(flat, w_ab, preferred_element_type=jnp.float32).reshape(
        tile_rows, tile_cols, 4 * hidden
    )
    row_live = (row_start + jnp.arange(tile_rows, dtype=jnp.int32) < lengths[0]).astype(jnp.float32)
    col_live = (col_start + jnp.arange(tile_cols, dtype=jnp.int32) < lengths[0]).astype(jnp.float32)
    pair_mask = (row_live[:, None] * col_live[None, :])[..., None]
    left = (pair_mask * jax.nn.sigmoid(proj[..., :hidden]) * proj[..., hidden : 2 * hidden]).astype(
        jnp.bfloat16
    )
    right = (
        pair_mask * jax.nn.sigmoid(proj[..., 2 * hidden : 3 * hidden]) * proj[..., 3 * hidden :]
    ).astype(jnp.bfloat16)
    left_major = jnp.transpose(left, (2, 0, 1))
    right_major = jnp.transpose(right, (2, 0, 1))
    column_rows = lax.all_gather(right_major, ("gx", "gz"), axis=1, tiled=True)
    right_mine = lax.all_to_all(column_rows, "gy", split_axis=1, concat_axis=2, tiled=True)
    triangle = jnp.einsum(
        "cik,cjk->cij",
        lax.all_gather(left_major, "gy", axis=2, tiled=True),
        right_mine,
        preferred_element_type=jnp.float32,
    )
    tri_norm = channel_norm(triangle, out_gain, out_bias).astype(jnp.bfloat16)
    gate = jax.nn.sigmoid(jnp.dot(flat, w_gate, preferred_element_type=jnp.float32)).reshape(
        tile_rows, tile_cols, width
    )
    projected = jnp.einsum("cij,cd->ijd", tri_norm, w_out, preferred_element_type=jnp.float32)
    return (gate * projected).astype(jnp.bfloat16)


def solution(mesh):
    in_specs = (P(("grp", "gx", "gz"), "gy", None), P("grp"), P(), P(), P(), P(), P(), P(), P())
    out_specs = P(("grp", "gx", "gz"), "gy", None)
    return jax.shard_map(body, mesh=mesh, in_specs=in_specs, out_specs=out_specs, check_vma=False)
```

profile of v0, /device:TPU:0, one launch (start us, length us, event | category | flops | bytes accessed | tf_op | source)
XLA Modules:
  0.0 898.8 jit_solution(9406988459465322010)
XLA Ops:
  7.4 3.8 convert_reduce_fusion
  11.2 6.0 fusion.5
  17.2 0.1 broadcast_multiply_fusion
  17.4 4.9 fusion.8
  22.3 13.1 %fusion.25 = f32[128,128,512]{2,1,0:T(8,128)} fusion(bf16[128,128,128]{2,1,0:T(8,128)(2,1)S(1)} %fusion.8, bf16[128,512]{1,0:T(8,128)(2,1)S(1)} %copy-done), kind=kOutput, calls=%fused_computation.34 | convolution fusion | flops 2147483648 | bytes 37879808 | tf_op jit(solution)/shard_map/dot_general | solution.py:28
  35.5 15.6 %fusion.22 = (bf16[128,128,128]{0,2,1:T(8,128)(2,1)}, bf16[128,128,128]{0,2,1:T(8,128)(2,1)}) fusion(f32[128,128,512]{2,1,0:T(8,128)} %fusion.25, f32[128,128]{1,0:T(8,128)S(1)} %broadcast_multiply_fusion), kind=kLoop, calls=%fused_computation.33 | loop fusion | flops 25165824 | bytes 42008576 | tf_op jit(solution)/shard_map/transpose | solution.py:41
  51.1 6.4 copy.13
  57.4 0.0 all-gather.5.cloned.1.call-update
  57.5 0.0 all-gather.3.cloned.1.call-start
  57.5 0.7 all-gather.3.cloned.1.call-update
  58.2 108.0 %all-gather.5.cloned.1.call-done = bf16[128,512,128]{2,0,1:T(8,128)(2,1)} async-done(((bf16[128,128,128]{2,0,1:T(8,128)(2,1)}), bf16[128,512,128]{2,0,1:T(8,128)(2,1)}) %all-gather.5.cloned.1.call-update) | async-done | bytes 16777232 | tf_op jit(solution)/shard_map/all_gather | solution.py:42
  166.2 7.3 all-to-all-start
  173.5 9.0 %fusion.2 = f32[16384,128]{1,0:T(8,128)} fusion(bf16[16384,128]{1,0:T(8,128)(2,1)} %bitcast.24, bf16[128,128]{1,0:T(8,128)(2,1)S(1)} %copy-done.10), kind=kOutput, calls=%fused_computation.3 | convolution fusion | flops 543162368 | bytes 12615680 | tf_op jit(solution)/shard_map/dot_general | solution.py:51
  182.5 580.3 %all-gather.3.cloned.1.call-done = bf16[128,128,512]{0,2,1:T(8,128)(2,1)} async-done(((bf16[128,128,128]{0,2,1:T(8,128)(2,1)}), bf16[128,128,512]{0,2,1:T(8,128)(2,1)}) %all-gather.3.cloned.1.call-update) | async-done | bytes 16777232 | tf_op jit(solution)/shard_map/all_gather | solution.py:46
  762.8 23.4 %copy.15 = bf16[128,128,512]{2,1,0:T(8,128)(2,1)} copy(bf16[128,128,512]{0,2,1:T(8,128)(2,1)} %all-gather.3.cloned.1.call-done) | data formatting | bytes 33554432 | tf_op jit(solution)/shard_map/all_gather | solution.py:46
  786.2 20.3 %all-to-all-done = bf16[128,512,128]{2,0,1:T(8,128)(2,1)} async-done(((bf16[128,512,128]{2,0,1:T(8,128)(2,1)}), bf16[128,512,128]{2,0,1:T(8,128)(2,1)}, u32[]{:S(2)}, u32[]{:S(2)}) %all-to-all-start) | async-done | bytes 16777248 | tf_op jit(solution)/shard_map/all_to_all | solution.py:43
  806.5 22.0 %copy.22 = bf16[128,4,128,128]{3,1,2,0:T(4,128)(2,1)} copy(bf16[128,4,128,128]{3,0,2,1:T(8,128)(2,1)} %bitcast.6) | data formatting | bytes 33554432 | tf_op jit(solution)/shard_map/all_to_all | solution.py:43
  828.6 24.9 %all_to_all.16 = bf16[128,128,512]{2,1,0:T(8,128)(2,1)} reshape(bf16[128,128,4,128]{3,2,1,0:T(4,128)(2,1)} %bitcast.23) | data formatting | bytes 33554432 | tf_op jit(solution)/shard_map/all_to_all | solution.py:43
  853.4 16.4 %fusion.28 = (f32[128,128]{1,0:T(8,128)S(1)}, f32[128,128,128]{2,1,0:T(8,128)}) fusion(bf16[128,128,512]{2,1,0:T(8,128)(2,1)} %copy.15, bf16[128,128,512]{2,1,0:T(8,128)(2,1)} %all_to_all.16), kind=kOutput, calls=%fused_computation.44 | convolution fusion | flops 2149564416 | bytes 42008576 | tf_op jit(solution)/shard_map/cik,cjk->cij/dot_general | solution.py:44
  869.8 4.4 multiply_reduce_fusion
  874.3 1.3 copy-done.2
  875.6 2.0 add_convert_fusion
  877.6 0.0 copy-start.1
  877.6 14.4 %multiply_convert_fusion = bf16[128,128,128]{2,1,0:T(8,128)(2,1)} fusion(f32[128,128,128]{2,1,0:T(8,128)} %bitcast.25, bf16[128,128,128]{2,1,0:T(8,128)(2,1)S(1)} %add_convert_fusion, bf16[128,128]{1,0:T(8,128)(2,1)S(1)} %copy-done.5), kind=kOutput, calls=%fused_computation.27 | convolution fusion | flops 541065216 | bytes 16809984 | tf_op jit(solution)/shard_map/cij,cd->ijd/dot_general | solution.py:54
  (26 shorter events, 0.1 us)
Async XLA Ops:
  6.5 15.8 %copy-start = (bf16[128,512]{1,0:T(8,128)(2,1)S(1)}, bf16[128,512]{1,0:T(8,128)(2,1)}, u32[]{:S(2)}) copy-start(bf16[128,512]{1,0:T(8,128)(2,1)} %param.13) | copy-start | bytes 393220
  6.5 10.8 %copy-start.7 = (f32[128]{0:T(128)S(1)}, f32[128]{0:T(128)}, u32[]{:S(2)}) copy-start(f32[128]{0:T(128)} %param.11) | copy-start | bytes 1540
  6.5 10.8 %copy-start.6 = (f32[128]{0:T(128)S(1)}, f32[128]{0:T(128)}, u32[]{:S(2)}) copy-start(f32[128]{0:T(128)} %param.12) | copy-start | bytes 1540
  6.5 159.7 %all-gather.5.cloned.1.call-start = ((), (), s32[]{:S(2)}) async-start(), calls=%async_computation.2 | async-start | bytes 20971520 | tf_op jit(solution)/shard_map/all_gather | solution.py:42
  6.6 10.8 %copy-start.3 = (bf16[128,128,128]{2,1,0:T(8,128)(2,1)S(1)}, bf16[128,128,128]{2,1,0:T(8,128)(2,1)}, u32[]{:S(2)}) copy-start(bf16[128,128,128]{2,1,0:T(8,128)(2,1)} %param.9) | copy-start | bytes 12582916
  22.3 13.2 %copy-start.4 = (bf16[128,128,128]{2,1,0:T(8,128)(2,1)}, bf16[128,128,128]{2,1,0:T(8,128)(2,1)S(1)}, u32[]{:S(2)}) copy-start(bf16[128,128,128]{2,1,0:T(8,128)(2,1)S(1)} %fusion.8) | copy-start | bytes 12582916
  57.5 705.3 %all-gather.3.cloned.1.call-start = ((), (), s32[]{:S(2)}) async-start(), calls=%async_computation.1 | async-start | bytes 20971520 | tf_op jit(solution)/shard_map/all_gather | solution.py:46
  58.2 115.3 %copy-start.10 = (bf16[128,128]{1,0:T(8,128)(2,1)S(1)}, bf16[128,128]{1,0:T(8,128)(2,1)}, u32[]{:S(2)}) copy-start(bf16[128,128]{1,0:T(8,128)(2,1)} %param.14) | copy-start | bytes 98308
  166.2 640.3 %all-to-all-start = ((bf16[128,512,128]{2,0,1:T(8,128)(2,1)}), bf16[128,512,128]{2,0,1:T(8,128)(2,1)}, u32[]{:S(2)}, u32[]{:S(2)}) async-start(bf16[128,512,128]{2,0,1:T(8,128)(2,1)} %all-gather.5.cloned.1.call-done), calls=%async_computation | async-start | bytes 33554432 | tf_op jit(solution)/shard_map/all_to_all | solution.py:43
  869.8 5.8 copy-start.2
  869.8 5.8 copy-start.8
  869.8 5.8 copy-start.9
  874.2 3.3 copy-start.5
  877.6 14.4 %copy-start.1 = (bf16[128,512]{1,0:T(8,128)(2,1)S(1)}, bf16[128,512]{1,0:T(8,128)(2,1)}, u32[]{:S(2)}) copy-start(bf16[128,512]{1,0:T(8,128)(2,1)} %param.13) | copy-start | bytes 393220
Sparse Core Ops, SparseCore 0:
  57.6 108.6 all-gather.4
  167.8 594.9 all-gather.2
where the time goes:
time: 900 us; the launch traced here: 899 us
  waiting for transfers between devices  709 us (79%)
  local copies, waits for them, and re-layouts  78 us (9%)
  matrix products  52.9 us (6%)
  other arithmetic  36.9 us (4%)
  between operations  14.4 us (2%)
    all_gather x1, waiting for transfers between devices, body(): lax.all_gather(left_major, 'gy', axis=2, tiled=True)  580 us
    all_gather x1, waiting for transfers between devices, body(): column_rows = lax.all_gather(right_major, ('gx', 'gz'), axis=1, tiled=True)  108 us
    all_to_all x2, local copies, waits for them, and re-layouts, body(): lax.all_to_all(column_rows, 'gy', split_axis=1, concat_axis=2, tiled=True)  46.9 us
    all_gather x1, local copies, waits for them, and re-layouts, body(): lax.all_gather(left_major, 'gy', axis=2, tiled=True)  23.4 us
    all_to_all x1, waiting for transfers between devices, body(): lax.all_to_all(column_rows, 'gy', split_axis=1, concat_axis=2, tiled=True)  20.3 us
  transfers between devices with their start and end apart: 3, of which 3 were waited for; matrix products, arithmetic and copies ran while one was open for 4% of the time, Pallas kernels for 0%

commit v1 on v0

--- a/solution.py
+++ b/solution.py
@@ -18,6 +18,23 @@
 
 
 def body(pair, lengths, ln_gain, ln_bias, w_ab, w_gate, out_gain, out_bias, w_out):
+
+    def feed_lines(in_array, lane_axis, local_block):
+        t_next = lax.axis_size(lane_axis)
+        long_array = lax.axis_index(lane_axis)
+        small, back = (t_next, long_array)
+        cards = []
+        for to_i in range(small):
+            cards.append((to_i, (to_i - 1) % small))
+        x_new = in_array
+        o_now = in_array.shape[2]
+        right_arr = local_block(x_new, back * o_now)
+        for pp in range(1, small):
+            x_new = lax.ppermute(x_new, lane_axis, cards)
+            extra = local_block(x_new, (back + pp) % small * o_now)
+            right_arr = right_arr + extra
+        return right_arr
+
     tile_rows, tile_cols, width = pair.shape
     hidden = w_out.shape[0]
     row_start = lax.axis_index(("gx", "gz")) * tile_rows
@@ -41,11 +58,15 @@
     right_major = jnp.transpose(right, (2, 0, 1))
     column_rows = lax.all_gather(right_major, ("gx", "gz"), axis=1, tiled=True)
     right_mine = lax.all_to_all(column_rows, "gy", split_axis=1, concat_axis=2, tiled=True)
-    triangle = jnp.einsum(
-        "cik,cjk->cij",
-        lax.all_gather(left_major, "gy", axis=2, tiled=True),
-        right_mine,
-        preferred_element_type=jnp.float32,
+    triangle = feed_lines(
+        left_major,
+        "gy",
+        lambda own_block, start: jnp.einsum(
+            "cik,cjk->cij",
+            own_block,
+            lax.dynamic_slice_in_dim(right_mine, start, own_block.shape[2], axis=2),
+            preferred_element_type=jnp.float32,
+        ),
     )
     tri_norm = channel_norm(triangle, out_gain, out_bias).astype(jnp.bfloat16)
     gate = jax.nn.sigmoid(jnp.dot(flat, w_gate, preferred_element_type=jnp.float32)).reshape(

time: 900 us -> 937 us (1.041)
  matrix products: 52.9 us -> 77.1 us
    ppermute x0 -> x3, waiting for transfers between devices: none -> 600 us  [feed_lines(): x_new = lax.ppermute(x_new, lane_axis, cards)]
    all_gather x1 -> x0, waiting for transfers between devices: 580 us -> none  [body(): lax.all_gather(left_major, 'gy', axis=2, tiled=True)]
    dot_general x1 -> x4, matrix products: 16.4 us -> 41.9 us  [body(): jnp.einsum('cik,cjk->cij', own_block, lax.dynamic_slice_in_dim(right_mine...]
    all_gather x1 -> x0, local copies, waits for them, and re-layouts: 23.4 us -> none  [body(): lax.all_gather(left_major, 'gy', axis=2, tiled=True)]
    all_to_all x1, waiting for transfers between devices: 20.3 us -> 0.01 us  [body(): lax.all_to_all(column_rows, 'gy', split_axis=1, concat_axis=2, tiled=True)]
    ppermute x0 -> x3, local copies, waits for them, and re-layouts: none -> 20.2 us  [feed_lines(): x_new = lax.ppermute(x_new, lane_axis, cards)]
  transfers between devices with their start and end apart: 3 -> 5, of which waited for: 3 -> 4; matrix products, arithmetic and copies ran while one was open for 4% -> 4% of each run, Pallas kernels for 0% -> 0%
where the time goes in v1:
time: 937 us; the launch traced here: 935 us
  waiting for transfers between devices  709 us (76%)
  local copies, waits for them, and re-layouts  83.5 us (9%)
  matrix products  77.1 us (8%)
  other arithmetic  36.7 us (4%)
  starting transfers between devices  15 us (2%)
  between operations  14.4 us (2%)
    ppermute x3, waiting for transfers between devices, feed_lines(): x_new = lax.ppermute(x_new, lane_axis, cards)  600 us
    all_gather x1, waiting for transfers between devices, body(): column_rows = lax.all_gather(right_major, ('gx', 'gz'), axis=1, tiled=True)  109 us
    all_to_all x2, local copies, waits for them, and re-layouts, body(): lax.all_to_all(column_rows, 'gy', split_axis=1, concat_axis=2, tiled=True)  46.9 us
    dot_general x4, matrix products, body(): jnp.einsum('cik,cjk->cij', own_block, lax.dynamic_slice_in_dim(right_mine...  41.9 us
    ppermute x3, local copies, waits for them, and re-layouts, feed_lines(): x_new = lax.ppermute(x_new, lane_axis, cards)  20.2 us
  transfers between devices with their start and end apart: 5, of which 4 were waited for; matrix products, arithmetic and copies ran while one was open for 4% of the time, Pallas kernels for 0%

profile of v1, /device:TPU:0, one launch (start us, length us, event | category | flops | bytes accessed | tf_op | source)
XLA Modules:
  0.0 935.2 jit_solution(15680076525316108245)
XLA Ops:
  11.2 6.0 fusion.5
  17.4 4.9 fusion.8
  22.3 13.1 %fusion.35 = f32[128,128,512]{2,1,0:T(8,128)} fusion(bf16[128,128,128]{2,1,0:T(8,128)(2,1)S(1)} %fusion.8, bf16[128,512]{1,0:T(8,128)(2,1)S(1)} %copy-done), kind=kOutput, calls=%fused_computation.43 | convolution fusion | flops 2147483648 | bytes 37879808 | tf_op jit(solution)/shard_map/dot_general | solution.py:45
  35.4 15.4 %fusion.30 = (bf16[128,128,128]{0,2,1:T(8,128)(2,1)}, bf16[128,128,128]{0,2,1:T(8,128)(2,1)}) fusion(f32[128,128,512]{2,1,0:T(8,128)} %fusion.35, f32[128,128]{1,0:T(8,128)S(1)} %broadcast_multiply_fusion), kind=kLoop, calls=%fused_computation.42 | loop fusion | flops 25165824 | bytes 42008576 | tf_op jit(solution)/shard_map/transpose | solution.py:58
  50.8 6.4 copy.16
  57.2 108.8 %all-gather.2.cloned.1.call-done = bf16[128,512,128]{2,0,1:T(8,128)(2,1)} async-done(((bf16[128,128,128]{2,0,1:T(8,128)(2,1)}), bf16[128,512,128]{2,0,1:T(8,128)(2,1)}) %all-gather.2.cloned.1.call-update) | async-done | bytes 16777232 | tf_op jit(solution)/shard_map/all_gather | solution.py:59
  166.0 7.0 all-to-all-start
  176.8 356.7 %collective-permute-done = bf16[128,128,128]{0,2,1:T(8,128)(2,1)S(1)} collective-permute-done((bf16[128,128,128]{0,2,1:T(8,128)(2,1)}, bf16[128,128,128]{0,2,1:T(8,128)(2,1)S(1)}, u32[]{:S(2)}, u32[]{:S(2)}) %collective-permute-start) | collective-permute-done | bytes 4194336 | tf_op jit(solution)/shard_map/ppermute | solution.py:33
  535.5 4.2 collective-permute-start.1
  539.7 179.4 %collective-permute-done.1 = bf16[128,128,128]{0,2,1:T(8,128)(2,1)} collective-permute-done((bf16[128,128,128]{0,2,1:T(8,128)(2,1)S(1)}, bf16[128,128,128]{0,2,1:T(8,128)(2,1)}, u32[]{:S(2)}, u32[]{:S(2)}) %collective-permute-start.1) | collective-permute-done | bytes 4194336 | tf_op jit(solution)/shard_map/ppermute | solution.py:33
  719.1 6.7 copy.18
  725.8 7.8 fusion.2
  733.5 6.7 copy.19
  740.3 6.7 copy.20
  747.0 63.7 %collective-permute-done.2 = bf16[128,128,128]{0,2,1:T(8,128)(2,1)} collective-permute-done((bf16[128,128,128]{0,2,1:T(8,128)(2,1)}, bf16[128,128,128]{0,2,1:T(8,128)(2,1)}, u32[]{:S(2)}, u32[]{:S(2)}) %collective-permute-start.2) | collective-permute-done | bytes 4194336 | tf_op jit(solution)/shard_map/ppermute | solution.py:33
  810.7 6.7 copy.21
  817.4 22.0 %copy.28 = bf16[128,4,128,128]{3,1,2,0:T(4,128)(2,1)} copy(bf16[128,4,128,128]{3,0,2,1:T(8,128)(2,1)} %bitcast.6) | data formatting | bytes 33554432 | tf_op jit(solution)/shard_map/all_to_all | solution.py:60
  839.4 24.9 %all_to_all.16 = bf16[128,128,512]{2,1,0:T(8,128)(2,1)} reshape(bf16[128,128,4,128]{3,2,1,0:T(4,128)(2,1)} %bitcast.25) | data formatting | bytes 33554432 | tf_op jit(solution)/shard_map/all_to_all | solution.py:60
  864.3 10.1 %fusion.25 = f32[128,128,128]{2,1,0:T(8,128)} fusion(bf16[128,128,128]{2,1,0:T(8,128)(2,1)} %copy.19, bf16[128,128,512]{2,1,0:T(8,128)(2,1)} %all_to_all.16, s32[]{:T(128)S(6)} %select_n.29), kind=kOutput, calls=%fused_computation.37 | convolution fusion | flops 536870912 | bytes 16777220 | tf_op jit(solution)/shard_map/cik,cjk->cij/dot_general | solution.py:64
  874.5 8.6 fusion.23
  883.1 6.2 fusion.27
  889.4 16.9 %fusion.42 = (f32[128,128]{1,0:T(8,128)S(1)}, f32[128,128,128]{2,1,0:T(8,128)}) fusion(bf16[128,128,128]{2,1,0:T(8,128)(2,1)} %copy.21, bf16[128,128,512]{2,1,0:T(8,128)(2,1)} %all_to_all.16, s32[]{:T(128)S(6)} %select_n.33, f32[128,128,128]{2,1,0:T(8,128)} %fusion.23, f32[128,128,128]{2,1,0:T(8,128)} %fusion.27, f32[128,128,128]{2,1,0:T(8,128)} %fusion.25), kind=kOutput, calls=%fused_computation.57 | convolution fusion | flops 545243136 | bytes 42008580 | tf_op jit(solution)/shard_map/cik,cjk->cij/dot_general | solution.py:64
  906.2 4.4 multiply_reduce_fusion
  914.0 14.4 %multiply_convert_fusion = bf16[128,128,128]{2,1,0:T(8,128)(2,1)} fusion(f32[128,128,128]{2,1,0:T(8,128)} %bitcast.27, bf16[128,128,128]{2,1,0:T(8,128)(2,1)S(1)} %add_convert_fusion, bf16[128,128]{1,0:T(8,128)(2,1)S(1)} %copy-done.8), kind=kOutput, calls=%fused_computation.27 | convolution fusion | flops 541065216 | bytes 16809984 | tf_op jit(solution)/shard_map/cij,cd->ijd/dot_general | solution.py:75
  (41 shorter events, 13.1 us)
Async XLA Ops:
  6.5 15.8 %copy-start = (bf16[128,512]{1,0:T(8,128)(2,1)S(1)}, bf16[128,512]{1,0:T(8,128)(2,1)}, u32[]{:S(2)}) copy-start(bf16[128,512]{1,0:T(8,128)(2,1)} %param.13) | copy-start | bytes 393220
  6.5 10.8 %copy-start.10 = (f32[128]{0:T(128)S(1)}, f32[128]{0:T(128)}, u32[]{:S(2)}) copy-start(f32[128]{0:T(128)} %param.11) | copy-start | bytes 1540
  6.5 10.8 %copy-start.9 = (f32[128]{0:T(128)S(1)}, f32[128]{0:T(128)}, u32[]{:S(2)}) copy-start(f32[128]{0:T(128)} %param.12) | copy-start | bytes 1540
  6.5 159.5 %all-gather.2.cloned.1.call-start = ((), (), s32[]{:S(2)}) async-start(), calls=%async_computation.1 | async-start | bytes 20971520 | tf_op jit(solution)/shard_map/all_gather | solution.py:59
  6.6 10.8 %copy-start.4 = (bf16[128,128,128]{2,1,0:T(8,128)(2,1)S(1)}, bf16[128,128,128]{2,1,0:T(8,128)(2,1)}, u32[]{:S(2)}) copy-start(bf16[128,128,128]{2,1,0:T(8,128)(2,1)} %param.9) | copy-start | bytes 12582916
  22.3 13.1 %copy-start.5 = (bf16[128,128,128]{2,1,0:T(8,128)(2,1)}, bf16[128,128,128]{2,1,0:T(8,128)(2,1)S(1)}, u32[]{:S(2)}) copy-start(bf16[128,128,128]{2,1,0:T(8,128)(2,1)S(1)} %fusion.8) | copy-start | bytes 12582916
  166.0 651.4 %all-to-all-start = ((bf16[128,512,128]{2,0,1:T(8,128)(2,1)}), bf16[128,512,128]{2,0,1:T(8,128)(2,1)}, u32[]{:S(2)}, u32[]{:S(2)}) async-start(bf16[128,512,128]{2,0,1:T(8,128)(2,1)} %all-gather.2.cloned.1.call-done), calls=%async_computation | async-start | bytes 33554432 | tf_op jit(solution)/shard_map/all_to_all | solution.py:60
  173.0 552.8 %copy-start.13 = (bf16[128,128]{1,0:T(8,128)(2,1)S(1)}, bf16[128,128]{1,0:T(8,128)(2,1)}, u32[]{:S(2)}) copy-start(bf16[128,128]{1,0:T(8,128)(2,1)} %param.14) | copy-start | bytes 98308
  173.0 360.5 %collective-permute-start = (bf16[128,128,128]{0,2,1:T(8,128)(2,1)}, bf16[128,128,128]{0,2,1:T(8,128)(2,1)S(1)}, u32[]{:S(2)}, u32[]{:S(2)}) collective-permute-start(bf16[128,128,128]{0,2,1:T(8,128)(2,1)} %get-tuple-element.6), channel_id=1, source_target_pairs={{0,12},{4,0},{8,4},{12,8},{1,13},{5,1},{9,5},{13,9},{2,14},{6,2},{... | collective-permute-start | bytes 12582920 | tf_op jit(solution)/shard_map/ppermute | solution.py:33
  533.5 2.0 copy-start.7
  535.5 183.6 %collective-permute-start.1 = (bf16[128,128,128]{0,2,1:T(8,128)(2,1)S(1)}, bf16[128,128,128]{0,2,1:T(8,128)(2,1)}, u32[]{:S(2)}, u32[]{:S(2)}) collective-permute-start(bf16[128,128,128]{0,2,1:T(8,128)(2,1)S(1)} %collective-permute-done), channel_id=1, source_target_pairs={{0,12},{4,0},{8,4},{12,8},{1,13},{5,1},{9,5},{13,9},{2,14},{6,2},{... | collective-permute-start | bytes 12582920 | tf_op jit(solution)/shard_map/ppermute | solution.py:33
  719.1 91.6 %collective-permute-start.2 = (bf16[128,128,128]{0,2,1:T(8,128)(2,1)}, bf16[128,128,128]{0,2,1:T(8,128)(2,1)}, u32[]{:S(2)}, u32[]{:S(2)}) collective-permute-start(bf16[128,128,128]{0,2,1:T(8,128)(2,1)} %collective-permute-done.1), channel_id=1, source_target_pairs={{0,12},{4,0},{8,4},{12,8},{1,13},{5,1},{9,5},{13,9},{2,14},{6,2},{... | collective-permute-start | bytes 12582920 | tf_op jit(solution)/shard_map/ppermute | solution.py:33
  864.3 10.1 %copy-start.3 = (bf16[128,128,512]{2,1,0:T(8,128)(2,1)S(1)}, bf16[128,128,512]{2,1,0:T(8,128)(2,1)}, u32[]{:S(2)}) copy-start(bf16[128,128,512]{2,1,0:T(8,128)(2,1)} %all_to_all.16) | copy-start | bytes 50331652
  874.5 8.6 copy-start.6
  906.2 5.8 copy-start.2
  906.2 5.8 copy-start.11
  906.2 5.8 copy-start.12
  910.7 3.4 copy-start.8
  914.0 14.4 %copy-start.1 = (bf16[128,512]{1,0:T(8,128)(2,1)S(1)}, bf16[128,512]{1,0:T(8,128)(2,1)}, u32[]{:S(2)}) copy-start(bf16[128,512]{1,0:T(8,128)(2,1)} %param.13) | copy-start | bytes 393220
Sparse Core Ops, SparseCore 0:
  57.4 108.6 all-gather.1
